TPU v7x, 32 devices: a whole 2x2x4 slice. The times are simulated.
32 devices in a mesh: grp: 1, blk: 8 (over z, y), node: 4 (over x, core), pair: 1.
Axes of the slice: x: 2, y: 2, z: 4, core: 2. Of those that a mesh axis runs over, the one named last changes fastest.
Arguments:
- query: bfloat16 [4608, 1280], P(('grp', 'blk', 'node'), 'pair'), may hold values from -600 to 600
- key: bfloat16 [4608, 1280], P(('grp', 'blk', 'node'), 'pair'), may hold values from -25 to 25
- value: bfloat16 [4608, 1280], P(('grp', 'blk', 'node'), 'pair'), may hold values from -6 to 6
- out_weight: bfloat16 [1280, 1280], P('pair'), may hold values from -0.15625 to 0.15625
Outputs:
- mixed: bfloat16 [4608, 1280], P(('grp', 'blk', 'node', 'pair'))
All inputs are finite; a program needn't handle non-finite values.
Results may differ from a plain program's by a relative error of at most 0.011.
Values may be sent and summed in bfloat16 or wider, within the bound.
A program may use at most 128 MiB of HBM per device.

v0:
```python
import math

import jax
import jax.numpy as jnp
from jax import lax
from jax.sharding import PartitionSpec as P

HD = 64


lowest = -1e30


def block_rows(count):
    size = count
    while size > 1024 and size % 2 == 0:
        size = size // 2
    return size


def attend(carry, keys_piece, values_piece, queries):
    count = keys_piece.shape[0]
    size = block_rows(count)
    q_rows, heads, width = queries.shape
    scale = 1.0 / math.sqrt(width)

    def update(turn, state):
        peak, total, accum = state
        key_block = lax.dynamic_slice_in_dim(keys_piece, turn * size, size, 0).reshape(
            size, heads, width
        )
        value_block = lax.dynamic_slice_in_dim(values_piece, turn * size, size, 0).reshape(
            size, heads, width
        )
        scores = (
            jnp.einsum("qhd,khd->hqk", queries, key_block, preferred_element_type=jnp.float32)
            * scale
        )
        fresh = jnp.maximum(peak, jnp.max(scores, axis=2))
        expo = jnp.exp(scores - fresh[:, :, None])
        factor = jnp.exp(peak - fresh)
        total = total * factor + jnp.sum(expo, axis=2)
        weighted = jnp.einsum(
            "hqk,khd->qhd",
            expo.astype(jnp.bfloat16),
            value_block,
            preferred_element_type=jnp.float32,
        )
        accum = (accum.reshape(q_rows, heads, width) * factor.T[:, :, None] + weighted).reshape(
            q_rows, heads * width
        )
        return (fresh, total, accum)

    return lax.fori_loop(0, count // size, update, carry)


def start_state(heads, count, features):
    return (
        jnp.full((heads, count), lowest, jnp.float32),
        jnp.zeros((heads, count), jnp.float32),
        jnp.zeros((count, features), jnp.float32),
    )


def per_device(query, key, value, out_weight):
    rows, features = query.shape
    heads = features // HD
    gathered = lax.all_gather(query, "node", axis=0, tiled=True)
    count = gathered.shape[0]
    q_three = gathered.reshape(count, heads, HD)
    peak, total, accum = attend(
        start_state(heads, count, features),
        lax.all_gather(key, "blk", axis=0, tiled=True),
        lax.all_gather(value, "blk", axis=0, tiled=True),
        q_three,
    )
    nodes = lax.axis_size("node")
    acc_parts = accum.reshape(nodes, rows, features)
    peak_parts = peak.T.reshape(nodes, rows, heads)
    total_parts = total.T.reshape(nodes, rows, heads)
    acc_in = lax.all_to_all(acc_parts, "node", split_axis=0, concat_axis=0, tiled=True)
    peak_in = lax.all_to_all(peak_parts, "node", split_axis=0, concat_axis=0, tiled=True)
    total_in = lax.all_to_all(total_parts, "node", split_axis=0, concat_axis=0, tiled=True)
    sources = acc_in.shape[0]
    items = acc_in.shape[1]
    best = jnp.max(peak_in, axis=0)
    weight = jnp.exp(peak_in - best[None])
    summed = jnp.sum(weight * total_in, axis=0)
    joined = jnp.sum(acc_in.reshape(sources, items, heads, HD) * weight[:, :, :, None], axis=0)
    attn = (joined / summed[:, :, None]).reshape(items, features).astype(jnp.bfloat16)
    return lax.psum_scatter(
        jnp.dot(attn, out_weight, preferred_element_type=jnp.float32).astype(jnp.bfloat16),
        "pair",
        scatter_dimension=0,
        tiled=True,
    )


def solution(mesh):
    in_specs = (
        P(("grp", "blk", "node"), "pair"),
        P(("grp", "blk", "node"), "pair"),
        P(("grp", "blk", "node"), "pair"),
        P("pair", None),
    )
    out_specs = P(("grp", "blk", "node", "pair"), None)
    return jax.shard_map(
        per_device, mesh=mesh, in_specs=in_specs, out_specs=out_specs, check_vma=False
    )
```

profile of v0, /device:TPU:3, one launch (start us, length us, event | category | flops | bytes accessed | tf_op | source)
XLA Modules:
  0.0 321.6 jit_solution(2416669906681257392)
XLA Ops:
  8.8 19.7 %all-gather.6.cloned.1.call-done = bf16[576,1280]{1,0:T(8,128)(2,1)} async-done(((bf16[144,1280]{1,0:T(8,128)(2,1)}), bf16[576,1280]{1,0:T(8,128)(2,1)}) %all-gather.6.cloned.1.call-update) | async-done | bytes 1474576 | tf_op jit(solution)/shard_map/all_gather | solution.py:68
  31.2 56.5 %all-gather.4.cloned.1.call-done = bf16[1152,1280]{1,0:T(8,128)(2,1)} async-done(((bf16[144,1280]{1,0:T(8,128)(2,1)}), bf16[1152,1280]{1,0:T(8,128)(2,1)}) %all-gather.4.cloned.1.call-update) | async-done | bytes 2949136 | tf_op jit(solution)/shard_map/all_gather | solution.py:73
  87.7 58.8 %all-gather.8.cloned.1.call-done = bf16[1152,1280]{1,0:T(8,128)(2,1)} async-done(((bf16[144,1280]{1,0:T(8,128)(2,1)}), bf16[1152,1280]{1,0:T(8,128)(2,1)}) %all-gather.8.cloned.1.call-update) | async-done | bytes 2949136 | tf_op jit(solution)/shard_map/all_gather | solution.py:74
  148.4 106.3 %while.18 = (s32[]{:T(128)}, f32[20,576]{1,0:T(8,128)S(1)}, f32[20,576]{1,0:T(8,128)}, f32[576,1280]{0,1:T(8,128)}, bf16[1152,1280]{1,0:T(8,128)(2,1)}, /*index=...) while((s32[]{:T(128)}, f32[20,576]{1,0:T(8,128)S(1)}, ...), condition=%wide.region_3.0_spmd.clone, body=%wide.region_0.0_spmd.clone.sunk | while | flops 1753320960 | bytes 102850792 | solution.py:54
  148.4 3.7 %constant_dynamic-slice_fusion.3 = (bf16[576,1280]{1,0:T(8,128)(2,1)}, bf16[576,1280]{1,0:T(8,128)(2,1)}) fusion(bf16[1152,1280]{1,0:T(8,128)(2,1)} %get-tuple-element.277, s32[]{:T(128)S(6)} %select_n.10, bf16[1152,1280]{1,0:T(8,128)(2,1)} %get-tuple-element.275), kind=kLoop, calls=%fused_computation.14.clone.1 | loop fusion | bytes 5898244 | tf_op jit(solution)/shard_map/while/body/eval_jaxpr/dynamic_slice | solution.py:32
  152.0 2.7 copy.49
  154.7 15.7 %bitcast_reduce_fusion.3 = (f32[20,576]{1,0:T(8,128)S(1)}, f32[20,576,576]{2,1,0:T(8,128)}) fusion(bf16[576,20,64]{0,2,1:T(8,128)(2,1)} %bitcast.67, bf16[576,20,64]{0,2,1:T(8,128)(2,1)} %get-tuple-element.276), kind=kOutput, calls=%fused_computation.1.clone.1 | convolution fusion | flops 862606080 | bytes 29537280 | tf_op jit(solution)/shard_map/while/body/eval_jaxpr/qhd,khd->hqk/dot_general | solution.py:36
  170.4 10.4 %fusion.28 = f32[20,576]{1,0:T(8,128)S(1)} fusion(f32[20,576,576]{2,1,0:T(8,128)} %get-tuple-element.246, f32[20,576]{1,0:T(8,128)S(1)} %get-tuple-element.272), kind=kLoop, calls=%fused_computation.4.clone.1 | loop fusion | flops 19895040 | bytes 26634240 | tf_op jit(solution)/shard_map/while/body/eval_jaxpr/reduce_sum | solution.py:42
  180.9 2.7 copy.50
  183.5 18.0 %bitcast_add_fusion.2 = f32[576,20,64]{0,2,1:T(8,128)} fusion(f32[576,20,64]{0,2,1:T(8,128)} %bitcast.70, bf16[576,20,64]{0,2,1:T(8,128)(2,1)} %bitcast.69, f32[20,576,576]{2,1,0:T(8,128)} %get-tuple-element.246, f32[20,576]{1,0:T(8,128)S(1)} %get-tuple-element.272, f32[576,20]{0,1:T(8,128)S(1)} %get-tuple-element.248), kind=kOutput, calls=%fused_computation.8.clone.1 | convolution fusion | flops 870727680 | bytes 34007040 | tf_op jit(solution)/shard_map/while/body/eval_jaxpr/hqk,khd->qhd/dot_general | solution.py:43
  201.5 3.7 %constant_dynamic-slice_fusion.3 = (bf16[576,1280]{1,0:T(8,128)(2,1)}, bf16[576,1280]{1,0:T(8,128)(2,1)}) fusion(bf16[1152,1280]{1,0:T(8,128)(2,1)} %get-tuple-element.277, s32[]{:T(128)S(6)} %select_n.10, bf16[1152,1280]{1,0:T(8,128)(2,1)} %get-tuple-element.275), kind=kLoop, calls=%fused_computation.14.clone.1 | loop fusion | bytes 5898244 | tf_op jit(solution)/shard_map/while/body/eval_jaxpr/dynamic_slice | solution.py:32
  205.2 2.7 copy.49
  207.8 15.7 %bitcast_reduce_fusion.3 = (f32[20,576]{1,0:T(8,128)S(1)}, f32[20,576,576]{2,1,0:T(8,128)}) fusion(bf16[576,20,64]{0,2,1:T(8,128)(2,1)} %bitcast.67, bf16[576,20,64]{0,2,1:T(8,128)(2,1)} %get-tuple-element.276), kind=kOutput, calls=%fused_computation.1.clone.1 | convolution fusion | flops 862606080 | bytes 29537280 | tf_op jit(solution)/shard_map/while/body/eval_jaxpr/qhd,khd->hqk/dot_general | solution.py:36
  223.5 10.4 %fusion.28 = f32[20,576]{1,0:T(8,128)S(1)} fusion(f32[20,576,576]{2,1,0:T(8,128)} %get-tuple-element.246, f32[20,576]{1,0:T(8,128)S(1)} %get-tuple-element.272), kind=kLoop, calls=%fused_computation.4.clone.1 | loop fusion | flops 19895040 | bytes 26634240 | tf_op jit(solution)/shard_map/while/body/eval_jaxpr/reduce_sum | solution.py:42
  234.0 2.7 copy.50
  236.7 18.0 %bitcast_add_fusion.2 = f32[576,20,64]{0,2,1:T(8,128)} fusion(f32[576,20,64]{0,2,1:T(8,128)} %bitcast.70, bf16[576,20,64]{0,2,1:T(8,128)(2,1)} %bitcast.69, f32[20,576,576]{2,1,0:T(8,128)} %get-tuple-element.246, f32[20,576]{1,0:T(8,128)S(1)} %get-tuple-element.272, f32[576,20]{0,1:T(8,128)S(1)} %get-tuple-element.248), kind=kOutput, calls=%fused_computation.8.clone.1 | convolution fusion | flops 870727680 | bytes 34007040 | tf_op jit(solution)/shard_map/while/body/eval_jaxpr/hqk,khd->qhd/dot_general | solution.py:43
  255.5 6.0 %all-to-all-start.1 = ((f32[4,1,2880]{2,1,0:T(1,128)}), f32[4,1,2880]{2,1,0:T(1,128)S(1)}, u32[]{:S(2)}, u32[]{:S(2)}) async-start(f32[4,1,2880]{2,1,0:T(1,128)} %reshape.60), calls=%async_computation.1 | async-start | bytes 94208 | tf_op jit(solution)/shard_map/all_to_all | solution.py:82
  263.2 5.5 %all-to-all-start.2 = ((f32[4,1,2880]{2,1,0:T(1,128)}), f32[4,1,2880]{2,1,0:T(1,128)S(1)}, u32[]{:S(2)}, u32[]{:S(2)}) async-start(f32[4,1,2880]{2,1,0:T(1,128)} %reshape.62), calls=%async_computation.2 | async-start | bytes 94208 | tf_op jit(solution)/shard_map/all_to_all | solution.py:83
  268.8 3.6 %copy.33 = f32[576,1280]{1,0:T(8,128)} copy(f32[576,1280]{0,1:T(8,128)} %get-tuple-element.131) | data formatting | bytes 5898240 | tf_op jit(solution)/shard_map/while | solution.py:54
  272.3 5.1 %all-to-all-start = ((f32[4,144,1280]{2,1,0:T(8,128)}), f32[4,144,1280]{2,1,0:T(8,128)}, u32[]{:S(2)}, u32[]{:S(2)}) async-start(f32[4,144,1280]{2,1,0:T(8,128)} %bitcast.72), calls=%async_computation | async-start | bytes 5898240 | tf_op jit(solution)/shard_map/all_to_all | solution.py:81
  282.1 5.3 %mul.59 = f32[4,144,20,64]{3,2,1,0:T(8,128)} broadcast(f32[4,144,20]{2,1,0:T(8,128)} %copy.35), dimensions={0,1,2} | broadcast | bytes 2995200 | tf_op jit(solution)/shard_map/mul | solution.py:89
  287.4 6.4 %mul.60 = f32[4,144,1280]{2,1,0:T(8,128)} reshape(f32[4,144,20,64]{3,2,1,0:T(8,128)} %mul.59) | data formatting | bytes 5898240 | tf_op jit(solution)/shard_map/mul | solution.py:89
  298.3 12.2 %all-to-all-done = f32[4,144,1280]{2,1,0:T(8,128)} async-done(((f32[4,144,1280]{2,1,0:T(8,128)}), f32[4,144,1280]{2,1,0:T(8,128)}, u32[]{:S(2)}, u32[]{:S(2)}) %all-to-all-start) | async-done | bytes 2949152 | tf_op jit(solution)/shard_map/all_to_all | solution.py:81
  310.4 3.2 multiply_reduce_fusion
  (48 shorter events, 20.1 us)
Async XLA Ops:
  6.5 307.1 %copy-start = (bf16[1280,1280]{1,0:T(8,128)(2,1)S(1)}, bf16[1280,1280]{1,0:T(8,128)(2,1)}, u32[]{:S(2)}) copy-start(bf16[1280,1280]{1,0:T(8,128)(2,1)} %param.9) | copy-start | bytes 9830404
  6.5 22.0 %all-gather.6.cloned.1.call-start = ((), (), s32[]{:S(2)}) async-start(), calls=%async_computation.4 | async-start | bytes 1843200 | tf_op jit(solution)/shard_map/all_gather | solution.py:68
  7.3 80.4 %all-gather.4.cloned.1.call-start = ((), (), s32[]{:S(2)}) async-start(), calls=%async_computation.3 | async-start | bytes 3317760 | tf_op jit(solution)/shard_map/all_gather | solution.py:73
  8.0 138.5 %all-gather.8.cloned.1.call-start = ((), (), s32[]{:S(2)}) async-start(), calls=%async_computation.5 | async-start | bytes 3317760 | tf_op jit(solution)/shard_map/all_gather | solution.py:74
  170.4 10.4 %copy-start.1 = (f32[20,576]{1,0:T(8,128)S(1)}, f32[20,576]{1,0:T(8,128)}, u32[]{:S(2)}) copy-start(f32[20,576]{1,0:T(8,128)} %get-tuple-element.262) | copy-start | bytes 138244 | tf_op jit(solution)/shard_map/while
  180.8 20.7 %copy-start.2 = (f32[20,576]{1,0:T(8,128)}, f32[20,576]{1,0:T(8,128)S(1)}, u32[]{:S(2)}) copy-start(f32[20,576]{1,0:T(8,128)S(1)} %fusion.29) | copy-start | bytes 138244 | tf_op jit(solution)/shard_map/while
  223.5 10.4 %copy-start.1 = (f32[20,576]{1,0:T(8,128)S(1)}, f32[20,576]{1,0:T(8,128)}, u32[]{:S(2)}) copy-start(f32[20,576]{1,0:T(8,128)} %get-tuple-element.262) | copy-start | bytes 138244 | tf_op jit(solution)/shard_map/while
  234.0 20.7 %copy-start.2 = (f32[20,576]{1,0:T(8,128)}, f32[20,576]{1,0:T(8,128)S(1)}, u32[]{:S(2)}) copy-start(f32[20,576]{1,0:T(8,128)S(1)} %fusion.29) | copy-start | bytes 138244 | tf_op jit(solution)/shard_map/while
  255.5 7.7 %all-to-all-start.1 = ((f32[4,1,2880]{2,1,0:T(1,128)}), f32[4,1,2880]{2,1,0:T(1,128)S(1)}, u32[]{:S(2)}, u32[]{:S(2)}) async-start(f32[4,1,2880]{2,1,0:T(1,128)} %reshape.60), calls=%async_computation.1 | async-start | bytes 94208 | tf_op jit(solution)/shard_map/all_to_all | solution.py:82
  263.2 9.1 %all-to-all-start.2 = ((f32[4,1,2880]{2,1,0:T(1,128)}), f32[4,1,2880]{2,1,0:T(1,128)S(1)}, u32[]{:S(2)}, u32[]{:S(2)}) async-start(f32[4,1,2880]{2,1,0:T(1,128)} %reshape.62), calls=%async_computation.2 | async-start | bytes 94208 | tf_op jit(solution)/shard_map/all_to_all | solution.py:83
  272.3 38.1 %all-to-all-start = ((f32[4,144,1280]{2,1,0:T(8,128)}), f32[4,144,1280]{2,1,0:T(8,128)}, u32[]{:S(2)}, u32[]{:S(2)}) async-start(f32[4,144,1280]{2,1,0:T(8,128)} %bitcast.72), calls=%async_computation | async-start | bytes 5898240 | tf_op jit(solution)/shard_map/all_to_all | solution.py:81
  310.4 3.2 %copy-start.3 = (f32[144,1280]{1,0:T(8,128)S(1)}, f32[144,1280]{1,0:T(8,128)}, u32[]{:S(2)}) copy-start(f32[144,1280]{1,0:T(8,128)} %div.12) | copy-start | bytes 2211844
Sparse Core Ops, SparseCore 0:
  8.9 19.5 all-gather.5
  30.7 56.9 all-gather.3
  89.9 56.5 all-gather.7
where the time goes:
time: 325 us; the launch traced here: 322 us
  waiting for transfers between devices  149 us (46%)
  matrix products  68.7 us (21%)
  local copies, waits for them, and re-layouts  47.4 us (15%)
  other arithmetic  26.3 us (8%)
  starting transfers between devices  16.6 us (5%)
  between operations  13.2 us (4%)
    all_gather x1, waiting for transfers between devices, per_device(): lax.all_gather(value, 'blk', axis=0, tiled=True)  58.8 us
    all_gather x1, waiting for transfers between devices, per_device(): lax.all_gather(key, 'blk', axis=0, tiled=True)  56.5 us
    dot_general x2, matrix products, update(): jnp.einsum('hqk,khd->qhd', expo.astype(jnp.bfloat16), value_block, prefer...  36 us
    dot_general x2, matrix products, update(): jnp.einsum('qhd,khd->hqk', queries, key_block, preferred_element_type=jnp...  31.3 us
    reduce_sum x2, other arithmetic, update(): total = total * factor + jnp.sum(expo, axis=2)  20.8 us
    all_gather x1, waiting for transfers between devices, per_device(): gathered = lax.all_gather(query, 'node', axis=0, tiled=True)  19.7 us
    dynamic_slice x4, local copies, waits for them, and re-layouts, update(): lax.dynamic_slice_in_dim(values_piece, turn * size, size, 0)  12.7 us
    all_to_all x1, waiting for transfers between devices, per_device(): lax.all_to_all(acc_parts, 'node', split_axis=0, concat_axis=0, tiled=True)  12.2 us
  transfers between devices with their start and end apart: 6, of which 4 were waited for; matrix products, arithmetic and copies ran while one was open for 9% of the time, Pallas kernels for 0%

commit v1 on v0

v1 whole, which is shorter than its diff:
```python
import functools
import math

import jax
import jax.numpy as jnp
from jax import lax
from jax.experimental import pallas as pl
from jax.experimental.pallas import tpu as pltpu
from jax.sharding import PartitionSpec as P

HD = 64
WIDE = 2 * HD


def groups_of(blk, heads):
    return max(g for g in range(1, blk + 1) if blk % g == 0 and heads % g == 0)


def kernel(
    G, B, N,
    q_ref, kv_ref, o_ref,
    qz, kvz, qbuf, kvbuf, vbuf, opack,
    z_send, z_recv, q_send, q_recv, kv_send, kv_recv, o_send, o_recv,
):
    H, R2, _ = q_ref.shape
    R = kv_ref.shape[1]
    hg = H // G
    PL = B // G
    inner = PL // N
    NS = kvbuf.shape[0]
    blk, node = lax.axis_index("blk"), lax.axis_index("node")
    z = blk // inner
    p = (blk % inner) * N + node

    def peer(zz, pp):
        return {"blk": zz * inner + pp // N, "node": pp % N}

    def remote(src, dst, send, recv, zz, pp):
        return pltpu.make_async_remote_copy(
            src_ref=src, dst_ref=dst, send_sem=send, recv_sem=recv,
            device_id=peer(zz, pp), device_id_type=pl.DeviceIdType.MESH,
        )

    def phase1(dz):
        g = lax.rem(z + dz, G)
        heads = pl.ds(g * hg, hg)
        return (
            remote(kv_ref.at[heads], kvz.at[dz - 1], z_send.at[dz - 1, 0], z_recv.at[dz - 1, 0], g, p),
            remote(q_ref.at[heads], qz.at[dz - 1], z_send.at[dz - 1, 1], z_recv.at[dz - 1, 1], g, p),
        )

    for dz in range(1, G):
        for c in phase1(dz):
            c.start()

    def first(pp):
        return (pp * H) // B

    def last(pp):
        return (pp * H + H - 1) // B

    def phase2(s, act):
        src_z = lax.rem(z - s + G, G)
        b = src_z * PL + p

        def kv_src(h):
            return kv_ref.at[z * hg + h] if s == 0 else kvz.at[s - 1, h]

        def one(dp, _):
            pp = lax.rem(p + dp, PL)
            f, l = first(pp), last(pp)
            for slot in range(NS):
                @pl.when(f + slot <= l)
                def _():
                    act(remote(kv_src(f + slot), kvbuf.at[slot, b], kv_send.at[s, dp, slot], kv_recv.at[slot, b], z, pp))
            return 0

        lax.fori_loop(1, PL, one, 0)
        for h in range(hg):
            n = h * B + b
            pp = n // H
            u = n - pp * H
            src = q_ref.at[z * hg + h] if s == 0 else qz.at[s - 1, h]

            @pl.when(pp != p)
            def _():
                act(remote(src, qbuf.at[u], q_send.at[s, h], q_recv.at[u], z, pp))

    def own(s):
        b = lax.rem(z - s + G, G) * PL + p
        for slot in range(NS):
            @pl.when(first(p) + slot <= last(p))
            def _():
                h = first(p) + slot
                src = kv_ref.at[z * hg + h] if s == 0 else kvz.at[s - 1, h]
                pltpu.make_async_copy(src, kvbuf.at[slot, b], kv_recv.at[slot, b]).start()
        for h in range(hg):
            n = h * B + b
            u = n - p * H
            src = q_ref.at[z * hg + h] if s == 0 else qz.at[s - 1, h]

            @pl.when(n // H == p)
            def _():
                pltpu.make_async_copy(src, qbuf.at[u], q_recv.at[u]).start()

    for s in range(G):
        if s > 0:
            for c in phase1(s):
                c.wait_recv()
        phase2(s, lambda c: c.start())
        own(s)

    def wait_q(u, _):
        pltpu.make_async_copy(qbuf.at[u], qbuf.at[u], q_recv.at[u]).wait()
        return 0

    lax.fori_loop(0, H, wait_q, 0)
    lanes = lax.broadcasted_iota(jnp.int32, (R, WIDE), 1)
    for slot in range(NS):
        @pl.when(first(p) + slot <= last(p))
        def _():
            def wait_kv(b, _):
                pltpu.make_async_copy(kvbuf.at[slot, b], kvbuf.at[slot, b], kv_recv.at[slot, b]).wait()
                vbuf[slot, b] = jnp.where(lanes < HD, jnp.ones((), vbuf.dtype), kvbuf[slot, b])
                return 0
            lax.fori_loop(0, B, wait_kv, 0)

    half = lax.broadcasted_iota(jnp.int32, (R2, WIDE), 1) < HD
    scale = 1.0 / math.sqrt(HD)

    def unit(u):
        n = p * H + u
        h = n // B
        slot = h - first(p)
        both = qbuf[u].astype(jnp.float32) * scale
        zero = jnp.zeros_like(both)
        queries = jnp.concatenate(
            [jnp.where(half, both, zero), jnp.where(half, pltpu.roll(both, HD, 1), zero)], axis=0
        ).astype(jnp.bfloat16)
        scores = lax.dot_general(
            queries, kvbuf[slot].reshape(B * R, WIDE), (((1,), (1,)), ((), ())),
            preferred_element_type=jnp.float32,
        )
        peak = jnp.max(scores, axis=1, keepdims=True)
        expo = jnp.exp(scores - peak).astype(jnp.bfloat16)
        weighted = jnp.dot(expo, vbuf[slot].reshape(B * R, WIDE), preferred_element_type=jnp.float32)
        turned = pltpu.roll(weighted, HD, 1)
        opack[u] = jnp.where(
            half, turned[:R2] / weighted[:R2], weighted[R2:] / turned[R2:]
        ).astype(opack.dtype)

    def give(u, act):
        n = p * H + u
        h = n // B
        b = n - h * B
        zz, pp = b // PL, lax.rem(b, PL)
        mine = jnp.logical_and(zz == z, pp == p)
        row = z * hg + h

        @pl.when(jnp.logical_not(mine))
        def _():
            act(remote(opack.at[u], o_ref.at[row], o_send.at[u], o_recv.at[row], zz, pp))

        return mine, row

    def turn(u, _):
        unit(u)
        mine, row = give(u, lambda c: c.start())

        @pl.when(mine)
        def _():
            pltpu.make_async_copy(opack.at[u], o_ref.at[row], o_recv.at[row]).start()

        return 0

    lax.fori_loop(0, H, turn, 0)

    for dz in range(1, G):
        for c in phase1(dz):
            c.wait_send()
    for s in range(G):
        phase2(s, lambda c: c.wait_send())

    def end(u, _):
        give(u, lambda c: c.wait_send())
        pltpu.make_async_copy(o_ref.at[u], o_ref.at[u], o_recv.at[u]).wait()
        return 0

    lax.fori_loop(0, H, end, 0)


def per_device(query, key, value, out_weight):
    R, features = query.shape
    H = features // HD
    R2 = R // 2
    nblk, N = lax.axis_size("blk"), lax.axis_size("node")
    B = nblk * N
    G = groups_of(nblk, H)
    hg = H // G
    NS = (H + B - 2) // B + 1
    q = query.reshape(2, R2, H, HD).transpose(2, 1, 0, 3).reshape(H, R2, WIDE)
    kv = jnp.concatenate(
        [key.reshape(R, H, HD), value.reshape(R, H, HD)], axis=2
    ).transpose(1, 0, 2)
    dma = pltpu.SemaphoreType.DMA
    bf = jnp.bfloat16
    out = pl.pallas_call(
        functools.partial(kernel, G, B, N),
        out_shape=jax.ShapeDtypeStruct((H, R2, WIDE), bf),
        in_specs=[pl.BlockSpec(memory_space=pltpu.VMEM)] * 2,
        out_specs=pl.BlockSpec(memory_space=pltpu.VMEM),
        scratch_shapes=[
            pltpu.VMEM((max(G - 1, 1), hg, R2, WIDE), bf),
            pltpu.VMEM((max(G - 1, 1), hg, R, WIDE), bf),
            pltpu.VMEM((H, R2, WIDE), bf),
            pltpu.VMEM((NS, B, R, WIDE), bf),
            pltpu.VMEM((NS, B, R, WIDE), bf),
            pltpu.VMEM((H, R2, WIDE), bf),
            dma((max(G - 1, 1), 2)),
            dma((max(G - 1, 1), 2)),
            dma((G, hg)),
            dma((H,)),
            dma((G, B // G, NS)),
            dma((NS, B)),
            dma((H,)),
            dma((H,)),
        ],
        compiler_params=pltpu.CompilerParams(
            has_side_effects=True, vmem_limit_bytes=60 * 1024 * 1024
        ),
        name="attention",
    )(q, kv)
    attn = out.reshape(H, R2, 2, HD).transpose(2, 1, 0, 3).reshape(R, features)
    return lax.psum_scatter(
        jnp.dot(attn, out_weight, preferred_element_type=jnp.float32).astype(jnp.bfloat16),
        "pair",
        scatter_dimension=0,
        tiled=True,
    )


def solution(mesh):
    in_specs = (
        P(("grp", "blk", "node"), "pair"),
        P(("grp", "blk", "node"), "pair"),
        P(("grp", "blk", "node"), "pair"),
        P("pair", None),
    )
    out_specs = P(("grp", "blk", "node", "pair"), None)
    return jax.shard_map(
        per_device, mesh=mesh, in_specs=in_specs, out_specs=out_specs, check_vma=False
    )
```

time: 325 us -> 109 us (0.34)
  waiting for transfers between devices: 149 us -> 0 us
  Pallas kernels: 0 us -> 79.9 us
  matrix products: 68.7 us -> 2.38 us
  other arithmetic: 26.3 us -> 2.4 us
  local copies, waits for them, and re-layouts: 47.4 us -> 23.9 us
  starting transfers between devices: 16.6 us -> 0 us
  between operations: 13.2 us -> 0.02 us
    all_gather x3 -> x0, waiting for transfers between devices: 135 us -> none  [the longest x1 58.8 us: per_device(): lax.all_gather(value, 'blk', axis=0, tiled=True)]
    pallas_call x0 -> x1, Pallas kernels: none -> 79.9 us  [per_device(): pl.pallas_call(functools.partial(kernel, G, B, N), out_shape=jax.ShapeDty...]
    dot_general x4 -> x0, matrix products: 67.3 us -> none  [the longest x2 36 us: update(): jnp.einsum('hqk,khd->qhd', expo.astype(jnp.bfloat16), value_block, prefer...]
    reduce_sum x4 -> x0, other arithmetic: 24.6 us -> none  [the longest x2 20.8 us: update(): total = total * factor + jnp.sum(expo, axis=2)]
    dynamic_slice x6 -> x0, local copies, waits for them, and re-layouts: 18 us -> none  [the longest x4 12.7 us: update(): lax.dynamic_slice_in_dim(values_piece, turn * size, size, 0)]
    reshape x4 -> x8, local copies, waits for them, and re-layouts: 1.07 us -> 18.8 us  [the longest x2 5.2 us: per_device(): attn = out.reshape(H, R2, 2, HD).transpose(2, 1, 0, 3).reshape(R, features)]
    all_to_all x3 -> x0, starting transfers between devices: 16.6 us -> none  [the longest x1 5.97 us: per_device(): lax.all_to_all(peak_parts, 'node', split_axis=0, concat_axis=0, tiled=True)]
    all_to_all x3 -> x0, waiting for transfers between devices: 12.2 us -> none  [the longest x1 12.2 us: per_device(): lax.all_to_all(acc_parts, 'node', split_axis=0, concat_axis=0, tiled=True)]
  transfers between devices with their start and end apart: 6 -> 0, of which waited for: 4 -> 0; matrix products, arithmetic and copies ran while one was open for 9% -> 0% of each run, Pallas kernels for 0% -> 0%
where the time goes in v1:
time: 109 us
  Pallas kernels  79.9 us (73%)
  local copies, waits for them, and re-layouts  23.9 us (22%)
  other arithmetic  2.4 us (2%)
  matrix products  2.38 us (2%)
    pallas_call x1, Pallas kernels, per_device(): pl.pallas_call(functools.partial(kernel, G, B, N), out_shape=jax.ShapeDty...  79.9 us
    reshape x2, local copies, waits for them, and re-layouts, per_device(): attn = out.reshape(H, R2, 2, HD).transpose(2, 1, 0, 3).reshape(R, features)  5.2 us
    reshape x2, local copies, waits for them, and re-layouts, per_device(): q = query.reshape(2, R2, H, HD).transpose(2, 1, 0, 3).reshape(H, R2, WIDE)  5.13 us
    reshape x2, local copies, waits for them, and re-layouts, per_device(): key.reshape(R, H, HD)  4.75 us
    reshape x2, local copies, waits for them, and re-layouts, per_device(): value.reshape(R, H, HD)  3.71 us
    transpose x1, local copies, waits for them, and re-layouts, per_device(): q = query.reshape(2, R2, H, HD).transpose(2, 1, 0, 3).reshape(H, R2, WIDE)  2.81 us
    transpose x1, other arithmetic, per_device(): kv = jnp.concatenate([key.reshape(R, H, HD), value.reshape(R, H, HD)], ax...  2.4 us
    dot_general x1, matrix products, per_device(): jnp.dot(attn, out_weight, preferred_element_type=jnp.float32)  2.38 us

profile of v1, /device:TPU:3, one launch (start us, length us, event | category | flops | bytes accessed | tf_op | source)
XLA Modules:
  0.0 108.6 jit_solution(12072436419418828922)
XLA Ops:
  0.0 0.0 copy-start
  0.0 2.6 %reshape.20 = bf16[144,20,64]{2,1,0:T(8,128)(2,1)} reshape(bf16[144,1280]{1,0:T(8,128)(2,1)} %param.5) | data formatting | bytes 737280 | tf_op jit(solution)/shard_map/reshape | solution.py:203
  2.6 2.2 %copy.7 = bf16[144,20,64]{2,0,1:T(8,128)(2,1)} copy(bf16[144,20,64]{2,1,0:T(8,128)(2,1)} %reshape.20) | data formatting | bytes 737280 | tf_op jit(solution)/shard_map/reshape | solution.py:203
  4.8 2.5 %reshape.21 = bf16[144,20,64]{2,1,0:T(8,128)(2,1)} reshape(bf16[144,1280]{1,0:T(8,128)(2,1)} %param.6) | data formatting | bytes 737280 | tf_op jit(solution)/shard_map/reshape | solution.py:203
  7.2 1.3 %copy.8 = bf16[144,20,64]{2,0,1:T(8,128)(2,1)S(1)} copy(bf16[144,20,64]{2,1,0:T(8,128)(2,1)} %reshape.21) | data formatting | bytes 737280 | tf_op jit(solution)/shard_map/reshape | solution.py:203
  8.5 2.4 %maximum_bitcast_fusion.kv_ref = bf16[20,144,128]{2,1,0:T(8,128)(2,1)} fusion(bf16[144,20,64]{2,0,1:T(8,128)(2,1)S(1)} %copy.8, bf16[144,20,64]{2,0,1:T(8,128)(2,1)} %copy.7), kind=kLoop, calls=%fused_computation.1 | loop fusion | flops 1474560 | bytes 1474560 | tf_op jit(solution)/shard_map/transpose | solution.py:204
  10.9 2.5 %reshape.18 = bf16[2,72,20,64]{3,2,1,0:T(8,128)(2,1)} reshape(bf16[144,1280]{1,0:T(8,128)(2,1)} %param.4) | data formatting | bytes 737280 | tf_op jit(solution)/shard_map/reshape | solution.py:201
  13.3 2.8 %copy.6 = bf16[20,72,2,64]{3,2,1,0:T(2,128)(2,1)} copy(bf16[20,72,2,64]{3,0,1,2:T(8,128)(2,1)} %bitcast.6) | data formatting | bytes 737280 | tf_op jit(solution)/shard_map/transpose | solution.py:201
  16.1 2.7 %reshape.19.q_ref = bf16[20,72,128]{2,1,0:T(8,128)(2,1)} reshape(bf16[20,72,2,64]{3,2,1,0:T(2,128)(2,1)} %copy.6) | data formatting | bytes 737280 | tf_op jit(solution)/shard_map/reshape | solution.py:201
  18.8 79.9 %attention.1 = bf16[20,72,128]{2,1,0:T(8,128)(2,1)} custom-call(bf16[20,72,128]{2,1,0:T(8,128)(2,1)} %reshape.19.q_ref, bf16[20,144,128]{2,1,0:T(8,128)(2,1)} %maximum_bitcast_fusion.kv_ref), custom_call_target="tpu_custom_call" | custom-call | tf_op jit(solution)/shard_map/attention/pallas_call | solution.py:207
  98.8 2.8 %reshape.22 = bf16[20,72,2,64]{3,2,1,0:T(2,128)(2,1)} reshape(bf16[20,72,128]{2,1,0:T(8,128)(2,1)} %attention.1) | data formatting | bytes 737280 | tf_op jit(solution)/shard_map/reshape | solution.py:233
  101.6 2.2 %copy.9 = bf16[2,72,20,64]{3,2,1,0:T(8,128)(2,1)} copy(bf16[2,72,20,64]{3,0,1,2:T(2,128)(2,1)} %bitcast.7) | data formatting | bytes 737280 | tf_op jit(solution)/shard_map/transpose | solution.py:233
  103.8 2.4 %reshape.23 = bf16[144,1280]{1,0:T(8,128)(2,1)} reshape(bf16[2,72,20,64]{3,2,1,0:T(8,128)(2,1)} %copy.9) | data formatting | bytes 737280 | tf_op jit(solution)/shard_map/reshape | solution.py:233
  106.2 0.0 copy-done
  106.2 2.4 %convolution_convert_fusion = bf16[144,1280]{1,0:T(8,128)(2,1)} fusion(bf16[144,1280]{1,0:T(8,128)(2,1)} %reshape.23, bf16[1280,1280]{1,0:T(8,128)(2,1)S(1)} %copy-done), kind=kOutput, calls=%fused_computation | convolution fusion | flops 472043520 | bytes 4014080 | tf_op jit(solution)/shard_map/dot_general | solution.py:235
Async XLA Ops:
  0.0 106.2 %copy-start = (bf16[1280,1280]{1,0:T(8,128)(2,1)S(1)}, bf16[1280,1280]{1,0:T(8,128)(2,1)}, u32[]{:S(2)}) copy-start(bf16[1280,1280]{1,0:T(8,128)(2,1)} %param.7) | copy-start | bytes 9830404

commit v2 on v1

v2 whole, which is shorter than its diff:
```python
import functools
import math

import jax
import jax.numpy as jnp
from jax import lax
from jax.experimental import pallas as pl
from jax.experimental.pallas import tpu as pltpu
from jax.sharding import PartitionSpec as P

HD = 64
WIDE = 2 * HD


def groups_of(blk, heads):
    return max(g for g in range(1, blk + 1) if blk % g == 0 and heads % g == 0)


def kernel(
    G, B, N,
    query_ref, key_ref, value_ref, weight_ref, mixed_ref,
    qp, kvp, qz, kvz, qbuf, kvbuf, vbuf, qfull, peaks, accum, opack, oin, attn, weight,
    z_send, z_recv, q_send, q_recv, kv_send, kv_recv, o_send, o_recv, w_sem,
):
    H, R2, _ = qp.shape
    R = kvp.shape[1]
    hg = H // G
    PL = B // G
    inner = PL // N
    NS = kvbuf.shape[0]
    C = math.gcd(H, B)
    blk, node = lax.axis_index("blk"), lax.axis_index("node")
    z = blk // inner
    p = (blk % inner) * N + node
    bf, f32 = jnp.bfloat16, jnp.float32

    load_weight = pltpu.make_async_copy(weight_ref, weight, w_sem)
    load_weight.start()

    def peer(zz, pp):
        return {"blk": zz * inner + pp // N, "node": pp % N}

    def remote(src, dst, send, recv, zz, pp):
        return pltpu.make_async_remote_copy(
            src_ref=src, dst_ref=dst, send_sem=send, recv_sem=recv,
            device_id=peer(zz, pp), device_id_type=pl.DeviceIdType.MESH,
        )

    half = lax.broadcasted_iota(jnp.int32, (R2, WIDE), 1) < HD
    wide_half = lax.broadcasted_iota(jnp.int32, (R, WIDE), 1) < HD

    for pair in range(H // 2):
        columns = slice(pair * WIDE, (pair + 1) * WIDE)
        block = query_ref[:, columns].astype(f32)
        turned = pltpu.roll(block, HD, 1)
        qp[2 * pair] = jnp.where(half, block[:R2], turned[R2:]).astype(bf)
        qp[2 * pair + 1] = jnp.where(half, turned[:R2], block[R2:]).astype(bf)
    for pair in range(H // 2):
        columns = slice(pair * WIDE, (pair + 1) * WIDE)
        keys = key_ref[:, columns].astype(f32)
        values = value_ref[:, columns].astype(f32)
        kvp[2 * pair] = jnp.where(wide_half, keys, pltpu.roll(values, HD, 1)).astype(bf)
        kvp[2 * pair + 1] = jnp.where(wide_half, pltpu.roll(keys, HD, 1), values).astype(bf)

    def phase1(dz, part):
        g = lax.rem(z + dz, G)
        src, dst = ((qp, qz), (kvp, kvz))[part]
        return remote(
            src.at[pl.ds(g * hg, hg)], dst.at[dz - 1], z_send.at[dz - 1, part], z_recv.at[dz - 1, part], g, p
        )

    for part in range(2):
        for dz in range(1, G):
            phase1(dz, part).start()

    def first(pp):
        return (pp * H) // B

    def last(pp):
        return (pp * H + H - 1) // B

    def plane(s):
        return lax.rem(z - s + G, G)

    def q_src(s, h):
        return qp.at[z * hg + h] if s == 0 else qz.at[s - 1, h]

    def kv_src(s, h):
        return kvp.at[z * hg + h] if s == 0 else kvz.at[s - 1, h]

    def share_q(s, act):
        b = plane(s) * PL + p
        for h in range(hg):
            n = h * B + b
            pp = n // H
            u = n - pp * H

            @pl.when(pp != p)
            def _():
                act(remote(q_src(s, h), qbuf.at[u], q_send.at[s, h], q_recv.at[u], z, pp))

    def own_q(s):
        b = plane(s) * PL + p
        for h in range(hg):
            n = h * B + b

            @pl.when(n // H == p)
            def _():
                pltpu.make_async_copy(q_src(s, h), qbuf.at[n - p * H], q_recv.at[n - p * H]).start()

    def share_kv(s, act):
        b = plane(s) * PL + p

        def one(dp, _):
            pp = lax.rem(p + dp, PL)
            for slot in range(NS):
                @pl.when(first(pp) + slot <= last(pp))
                def _():
                    act(remote(
                        kv_src(s, first(pp) + slot), kvbuf.at[slot, b],
                        kv_send.at[s, dp, slot], kv_recv.at[slot, b], z, pp,
                    ))
            return 0

        lax.fori_loop(1, PL, one, 0)

    def own_kv(s):
        b = plane(s) * PL + p
        for slot in range(NS):
            @pl.when(first(p) + slot <= last(p))
            def _():
                pltpu.make_async_copy(kv_src(s, first(p) + slot), kvbuf.at[slot, b], kv_recv.at[slot, b]).start()

    start = lambda c: c.start()
    share_q(0, start)
    own_q(0)
    share_kv(0, start)
    own_kv(0)
    for s in range(1, G):
        phase1(s, 0).wait_recv()
        share_q(s, start)
        own_q(s)

    scale = 1.0 / math.sqrt(HD)

    def take_q(u, _):
        pltpu.make_async_copy(qbuf.at[u], qbuf.at[u], q_recv.at[u]).wait()
        both = qbuf[u].astype(f32) * scale
        zero = jnp.zeros_like(both)
        qfull[u] = jnp.concatenate(
            [jnp.where(half, both, zero), jnp.where(half, pltpu.roll(both, HD, 1), zero)], axis=0
        ).astype(bf)
        return 0

    def take_kv(s):
        for slot in range(NS):
            @pl.when(first(p) + slot <= last(p))
            def _():
                def one(i, _):
                    b = plane(s) * PL + i
                    pltpu.make_async_copy(kvbuf.at[slot, b], kvbuf.at[slot, b], kv_recv.at[slot, b]).wait()
                    vbuf[slot, i] = jnp.where(wide_half, jnp.ones((), bf), kvbuf[slot, b])
                    return 0
                lax.fori_loop(0, PL, one, 0)

    def give(u, act):
        n = p * H + u
        h = n // B
        b = n - h * B
        zz, pp = b // PL, lax.rem(b, PL)
        mine = jnp.logical_and(zz == z, pp == p)
        row = z * hg + h

        @pl.when(jnp.logical_not(mine))
        def _():
            act(remote(opack.at[u], oin.at[row], o_send.at[u], o_recv.at[row], zz, pp))

        return mine, row

    def attend(s, t):
        slot = (p * H + t * C) // B - first(p)
        units = pl.ds(t * C, C)
        queries = qfull[units].reshape(C * R, WIDE)
        keys = kvbuf[slot, pl.ds(plane(s) * PL, PL)].reshape(PL * R, WIDE)
        scores = lax.dot_general(
            queries, keys, (((1,), (1,)), ((), ())), preferred_element_type=f32
        )
        peak = jnp.max(scores, axis=1, keepdims=True)
        if s > 0:
            before = peaks[units].reshape(C * R, WIDE)
            peak = jnp.maximum(before[:, :1], peak)
        expo = jnp.exp(scores - peak).astype(bf)
        total = jnp.dot(expo, vbuf[slot].reshape(PL * R, WIDE), preferred_element_type=f32)
        if s > 0:
            total = total + accum[units].reshape(C * R, WIDE) * jnp.exp(before - peak)
        if s < G - 1:
            peaks[units] = jnp.broadcast_to(peak, (C * R, WIDE)).reshape(C, R, WIDE)
            accum[units] = total.reshape(C, R, WIDE)
            return
        turned = pltpu.roll(total, HD, 1)
        for i in range(C):
            low, high = slice(i * R, i * R + R2), slice(i * R + R2, (i + 1) * R)
            opack[t * C + i] = jnp.where(
                half, turned[low] / total[low], total[high] / turned[high]
            ).astype(bf)
        for i in range(C):
            u = t * C + i
            mine, row = give(u, start)

            @pl.when(mine)
            def _():
                pltpu.make_async_copy(opack.at[u], oin.at[row], o_recv.at[row]).start()

    for s in range(G):
        if s + 1 < G:
            phase1(s + 1, 1).wait_recv()
            share_kv(s + 1, start)
            own_kv(s + 1)
        if s == 0:
            lax.fori_loop(0, H, take_q, 0)
        take_kv(s)

        def turn(t, _):
            attend(s, t)
            return 0

        lax.fori_loop(0, H // C, turn, 0)

    for dz in range(1, G):
        for part in range(2):
            phase1(dz, part).wait_send()
    for s in range(G):
        share_q(s, lambda c: c.wait_send())
        share_kv(s, lambda c: c.wait_send())

    def end(u, _):
        give(u, lambda c: c.wait_send())
        pltpu.make_async_copy(oin.at[u], oin.at[u], o_recv.at[u]).wait()
        return 0

    load_weight.wait()
    lax.fori_loop(0, H, end, 0)
    for pair in range(H // 2):
        even, odd = oin[2 * pair].astype(f32), oin[2 * pair + 1].astype(f32)
        attn[:, pair * WIDE:(pair + 1) * WIDE] = jnp.concatenate(
            [
                jnp.where(half, even, pltpu.roll(odd, HD, 1)),
                jnp.where(half, pltpu.roll(even, HD, 1), odd),
            ],
            axis=0,
        ).astype(bf)
    mixed_ref[...] = jnp.dot(attn[...], weight[...], preferred_element_type=f32).astype(bf)


def per_device(query, key, value, out_weight):
    R, features = query.shape
    H = features // HD
    R2 = R // 2
    nblk, N = lax.axis_size("blk"), lax.axis_size("node")
    B = nblk * N
    G = groups_of(nblk, H)
    hg = H // G
    NS = (H + B - 2) // B + 1
    dma = pltpu.SemaphoreType.DMA
    bf, f32 = jnp.bfloat16, jnp.float32
    vmem = pl.BlockSpec(memory_space=pltpu.VMEM)
    mixed = pl.pallas_call(
        functools.partial(kernel, G, B, N),
        out_shape=jax.ShapeDtypeStruct((R, out_weight.shape[1]), bf),
        in_specs=[vmem, vmem, vmem, pl.BlockSpec(memory_space=pl.ANY)],
        out_specs=vmem,
        scratch_shapes=[
            pltpu.VMEM((H, R2, WIDE), bf),
            pltpu.VMEM((H, R, WIDE), bf),
            pltpu.VMEM((max(G - 1, 1), hg, R2, WIDE), bf),
            pltpu.VMEM((max(G - 1, 1), hg, R, WIDE), bf),
            pltpu.VMEM((H, R2, WIDE), bf),
            pltpu.VMEM((NS, B, R, WIDE), bf),
            pltpu.VMEM((NS, B // G, R, WIDE), bf),
            pltpu.VMEM((H, R, WIDE), bf),
            pltpu.VMEM((H, R, WIDE), f32),
            pltpu.VMEM((H, R, WIDE), f32),
            pltpu.VMEM((H, R2, WIDE), bf),
            pltpu.VMEM((H, R2, WIDE), bf),
            pltpu.VMEM((R, features), bf),
            pltpu.VMEM(out_weight.shape, bf),
            dma((max(G - 1, 1), 2)),
            dma((max(G - 1, 1), 2)),
            dma((G, hg)),
            dma((H,)),
            dma((G, B // G, NS)),
            dma((NS, B)),
            dma((H,)),
            dma((H,)),
            dma(()),
        ],
        compiler_params=pltpu.CompilerParams(
            has_side_effects=True, vmem_limit_bytes=60 * 1024 * 1024
        ),
        name="attention",
    )(query, key, value, out_weight)
    return lax.psum_scatter(mixed, "pair", scatter_dimension=0, tiled=True)


def solution(mesh):
    in_specs = (
        P(("grp", "blk", "node"), "pair"),
        P(("grp", "blk", "node"), "pair"),
        P(("grp", "blk", "node"), "pair"),
        P("pair", None),
    )
    out_specs = P(("grp", "blk", "node", "pair"), None)
    return jax.shard_map(
        per_device, mesh=mesh, in_specs=in_specs, out_specs=out_specs, check_vma=False
    )
```

time: 109 us -> 79.6 us (0.73)
  local copies, waits for them, and re-layouts: 23.9 us -> 1.75 us
  Pallas kernels: 79.9 us -> 77.3 us
  other arithmetic: 2.4 us -> 0 us
  matrix products: 2.38 us -> 0 us
    reshape x8 -> x0, local copies, waits for them, and re-layouts: 18.8 us -> none  [the longest x2 5.2 us: per_device(): attn = out.reshape(H, R2, 2, HD).transpose(2, 1, 0, 3).reshape(R, features)]
    transpose x2 -> x0, local copies, waits for them, and re-layouts: 5.06 us -> none  [the longest x1 2.81 us: per_device(): q = query.reshape(2, R2, H, HD).transpose(2, 1, 0, 3).reshape(H, R2, WIDE)]
    pallas_call x1, Pallas kernels: 79.9 us -> 77.3 us  [per_device(): pl.pallas_call(functools.partial(kernel, G, B, N), out_shape=jax.ShapeDty...]
    transpose x1 -> x0, other arithmetic: 2.4 us -> none  [per_device(): kv = jnp.concatenate([key.reshape(R, H, HD), value.reshape(R, H, HD)], ax...]
    dot_general x1 -> x0, matrix products: 2.38 us -> none  [per_device(): jnp.dot(attn, out_weight, preferred_element_type=jnp.float32)]
    unnamed x2 -> x1, local copies, waits for them, and re-layouts: 0.01 us -> 1.75 us
where the time goes in v2:
time: 79.6 us; the launch traced here: 79 us
  Pallas kernels  77.3 us (97%)
  local copies, waits for them, and re-layouts  1.75 us (2%)
    pallas_call x1, Pallas kernels, per_device(): pl.pallas_call(functools.partial(kernel, G, B, N), out_shape=jax.ShapeDty...  77.3 us
    unnamed x1, local copies, waits for them, and re-layouts  1.75 us

profile of v2, /device:TPU:3, one launch (start us, length us, event | category | flops | bytes accessed | tf_op | source)
XLA Modules:
  0.0 79.0 jit_solution(2551219919701126095)
XLA Ops:
  0.0 77.3 %attention.1 = bf16[144,1280]{1,0:T(8,128)(2,1)} custom-call(bf16[144,1280]{1,0:T(8,128)(2,1)} %query_ref.1, bf16[144,1280]{1,0:T(8,128)(2,1)} %key_ref.1, bf16[144,1280]{1,0:T(8,128)(2,1)} %value_ref.1, bf16[1280,1280]{1,0:T(8,128)(2,1)} %weight_ref.1), custom_call_target="tpu_custom_call" | custom-call | tf_op jit(solution)/shard_map/attention/pallas_call | solution.py:267
  77.3 1.7 %copy.6 = bf16[144,1280]{1,0:T(8,128)(2,1)} copy(bf16[144,1280]{1,0:T(8,128)(2,1)} %attention.1) | data formatting | bytes 737280

commit v3 on v2

--- a/solution.py
+++ b/solution.py
@@ -19,7 +19,7 @@
 def kernel(
     G, B, N,
     query_ref, key_ref, value_ref, weight_ref, mixed_ref,
-    qp, kvp, qz, kvz, qbuf, kvbuf, vbuf, qfull, peaks, accum, opack, oin, attn, weight,
+    qp, kvp, kvz, qbuf, kvbuf, vbuf, qfull, peaks, accum, opack, oin, attn, weight,
     z_send, z_recv, q_send, q_recv, kv_send, kv_recv, o_send, o_recv, w_sem,
 ):
     H, R2, _ = qp.shape
@@ -36,6 +36,18 @@
 
     load_weight = pltpu.make_async_copy(weight_ref, weight, w_sem)
     load_weight.start()
+    barrier = pltpu.get_barrier_semaphore()
+    here = blk * N + node
+
+    def greet(d, _):
+        other = lax.rem(here + d, B)
+        pl.semaphore_signal(
+            barrier, inc=1, device_id={"blk": other // N, "node": lax.rem(other, N)},
+            device_id_type=pl.DeviceIdType.MESH,
+        )
+        return 0
+
+    lax.fori_loop(1, B, greet, 0)
 
     def peer(zz, pp):
         return {"blk": zz * inner + pp // N, "node": pp % N}
@@ -62,16 +74,41 @@
         kvp[2 * pair] = jnp.where(wide_half, keys, pltpu.roll(values, HD, 1)).astype(bf)
         kvp[2 * pair + 1] = jnp.where(wide_half, pltpu.roll(keys, HD, 1), values).astype(bf)
 
-    def phase1(dz, part):
+    pl.semaphore_wait(barrier, B - 1)
+
+    def send_q(i, act):
+        row = lax.rem((z + 1) * hg + i, H)
+        zz = row // hg
+        n = (row - zz * hg) * B + here
+        pp = n // H
+        u = n - pp * H
+        mine = jnp.logical_and(zz == z, pp == p)
+
+        @pl.when(jnp.logical_not(mine))
+        def _():
+            act(remote(qp.at[row], qbuf.at[u], q_send.at[row], q_recv.at[u], zz, pp))
+
+        return mine, row, u
+
+    def start_q(i, _):
+        mine, row, u = send_q(i, lambda c: c.start())
+
+        @pl.when(mine)
+        def _():
+            pltpu.make_async_copy(qp.at[row], qbuf.at[u], q_recv.at[u]).start()
+
+        return 0
+
+    lax.fori_loop(0, H, start_q, 0)
+
+    def phase1(dz):
         g = lax.rem(z + dz, G)
-        src, dst = ((qp, qz), (kvp, kvz))[part]
         return remote(
-            src.at[pl.ds(g * hg, hg)], dst.at[dz - 1], z_send.at[dz - 1, part], z_recv.at[dz - 1, part], g, p
+            kvp.at[pl.ds(g * hg, hg)], kvz.at[dz - 1], z_send.at[dz - 1], z_recv.at[dz - 1], g, p
         )
 
-    for part in range(2):
-        for dz in range(1, G):
-            phase1(dz, part).start()
+    for dz in range(1, G):
+        phase1(dz).start()
 
     def first(pp):
         return (pp * H) // B
@@ -79,37 +116,11 @@
     def last(pp):
         return (pp * H + H - 1) // B
 
-    def plane(s):
-        return lax.rem(z - s + G, G)
-
-    def q_src(s, h):
-        return qp.at[z * hg + h] if s == 0 else qz.at[s - 1, h]
-
     def kv_src(s, h):
         return kvp.at[z * hg + h] if s == 0 else kvz.at[s - 1, h]
 
-    def share_q(s, act):
-        b = plane(s) * PL + p
-        for h in range(hg):
-            n = h * B + b
-            pp = n // H
-            u = n - pp * H
-
-            @pl.when(pp != p)
-            def _():
-                act(remote(q_src(s, h), qbuf.at[u], q_send.at[s, h], q_recv.at[u], z, pp))
-
-    def own_q(s):
-        b = plane(s) * PL + p
-        for h in range(hg):
-            n = h * B + b
-
-            @pl.when(n // H == p)
-            def _():
-                pltpu.make_async_copy(q_src(s, h), qbuf.at[n - p * H], q_recv.at[n - p * H]).start()
-
     def share_kv(s, act):
-        b = plane(s) * PL + p
+        b = s * PL + p
 
         def one(dp, _):
             pp = lax.rem(p + dp, PL)
@@ -125,21 +136,15 @@
         lax.fori_loop(1, PL, one, 0)
 
     def own_kv(s):
-        b = plane(s) * PL + p
+        b = s * PL + p
         for slot in range(NS):
             @pl.when(first(p) + slot <= last(p))
             def _():
                 pltpu.make_async_copy(kv_src(s, first(p) + slot), kvbuf.at[slot, b], kv_recv.at[slot, b]).start()
 
     start = lambda c: c.start()
-    share_q(0, start)
-    own_q(0)
     share_kv(0, start)
     own_kv(0)
-    for s in range(1, G):
-        phase1(s, 0).wait_recv()
-        share_q(s, start)
-        own_q(s)
 
     scale = 1.0 / math.sqrt(HD)
 
@@ -152,16 +157,15 @@
         ).astype(bf)
         return 0
 
-    def take_kv(s):
+    def take_kv(low, high):
         for slot in range(NS):
             @pl.when(first(p) + slot <= last(p))
             def _():
-                def one(i, _):
-                    b = plane(s) * PL + i
+                def one(b, _):
                     pltpu.make_async_copy(kvbuf.at[slot, b], kvbuf.at[slot, b], kv_recv.at[slot, b]).wait()
-                    vbuf[slot, i] = jnp.where(wide_half, jnp.ones((), bf), kvbuf[slot, b])
+                    vbuf[slot, b] = jnp.where(wide_half, jnp.ones((), bf), kvbuf[slot, b])
                     return 0
-                lax.fori_loop(0, PL, one, 0)
+                lax.fori_loop(low * PL, high * PL, one, 0)
 
     def give(u, act):
         n = p * H + u
@@ -177,32 +181,42 @@
 
         return mine, row
 
-    def attend(s, t):
+    def attend(low, high, t):
         slot = (p * H + t * C) // B - first(p)
-        units = pl.ds(t * C, C)
-        queries = qfull[units].reshape(C * R, WIDE)
-        keys = kvbuf[slot, pl.ds(plane(s) * PL, PL)].reshape(PL * R, WIDE)
-        scores = lax.dot_general(
-            queries, keys, (((1,), (1,)), ((), ())), preferred_element_type=f32
-        )
-        peak = jnp.max(scores, axis=1, keepdims=True)
-        if s > 0:
-            before = peaks[units].reshape(C * R, WIDE)
-            peak = jnp.maximum(before[:, :1], peak)
-        expo = jnp.exp(scores - peak).astype(bf)
-        total = jnp.dot(expo, vbuf[slot].reshape(PL * R, WIDE), preferred_element_type=f32)
-        if s > 0:
-            total = total + accum[units].reshape(C * R, WIDE) * jnp.exp(before - peak)
-        if s < G - 1:
-            peaks[units] = jnp.broadcast_to(peak, (C * R, WIDE)).reshape(C, R, WIDE)
-            accum[units] = total.reshape(C, R, WIDE)
+        keys = kvbuf[slot, low * PL:high * PL].reshape((high - low) * PL * R, WIDE)
+        values = vbuf[slot, low * PL:high * PL].reshape((high - low) * PL * R, WIDE)
+
+        def product(c):
+            return lax.dot_general(
+                qfull[t * C + c], keys, (((1,), (1,)), ((), ())), preferred_element_type=f32
+            )
+
+        def soften(c, scores):
+            u = t * C + c
+            peak = jnp.max(scores, axis=1, keepdims=True)
+            if low > 0:
+                before = peaks[u]
+                peak = jnp.maximum(before[:, :1], peak)
+            expo = jnp.exp(scores - peak).astype(bf)
+            total = jnp.dot(expo, values, preferred_element_type=f32)
+            if low > 0:
+                total = total + accum[u] * jnp.exp(before - peak)
+            if high < G:
+                peaks[u] = jnp.broadcast_to(peak, (R, WIDE))
+                accum[u] = total
+                return
+            turned = pltpu.roll(total, HD, 1)
+            opack[u] = jnp.where(
+                half, turned[:R2] / total[:R2], total[R2:] / turned[R2:]
+            ).astype(bf)
+
+        scores = product(0)
+        for c in range(C):
+            ahead = product(c + 1) if c + 1 < C else None
+            soften(c, scores)
+            scores = ahead
+        if high < G:
             return
-        turned = pltpu.roll(total, HD, 1)
-        for i in range(C):
-            low, high = slice(i * R, i * R + R2), slice(i * R + R2, (i + 1) * R)
-            opack[t * C + i] = jnp.where(
-                half, turned[low] / total[low], total[high] / turned[high]
-            ).astype(bf)
         for i in range(C):
             u = t * C + i
             mine, row = give(u, start)
@@ -211,27 +225,46 @@
             def _():
                 pltpu.make_async_copy(opack.at[u], oin.at[row], o_recv.at[row]).start()
 
+    def relay(s):
+        if s < G:
+            phase1(s).wait_recv()
+            share_kv(s, start)
+            own_kv(s)
+
+    stages = [(s, s + 1) for s in range(min(G, 2))]
+    stages += [(s, min(s + 2, G)) for s in range(2, G, 2)]
+    turns = H // C
+    relay(1)
+    lax.fori_loop(0, H, take_q, 0)
+    for low, high in stages:
+        take_kv(low, high)
+
+        def turn(t, _):
+            attend(low, high, t)
+            return 0
+
+        if high == 2 and low == 1 and G > 3:
+            lax.fori_loop(0, turns // 2, turn, 0)
+            relay(3)
+            lax.fori_loop(turns // 2, turns, turn, 0)
+        else:
+            lax.fori_loop(0, turns, turn, 0)
+        if high == 1:
+            relay(2)
+        if high >= 2:
+            for s in range(high + 2, min(high + 4, G)):
+                relay(s)
+
+    for dz in range(1, G):
+        phase1(dz).wait_send()
     for s in range(G):
-        if s + 1 < G:
-            phase1(s + 1, 1).wait_recv()
-            share_kv(s + 1, start)
-            own_kv(s + 1)
-        if s == 0:
-            lax.fori_loop(0, H, take_q, 0)
-        take_kv(s)
-
-        def turn(t, _):
-            attend(s, t)
-            return 0
-
-        lax.fori_loop(0, H // C, turn, 0)
-
-    for dz in range(1, G):
-        for part in range(2):
-            phase1(dz, part).wait_send()
-    for s in range(G):
-        share_q(s, lambda c: c.wait_send())
         share_kv(s, lambda c: c.wait_send())
+
+    def end_q(i, _):
+        send_q(i, lambda c: c.wait_send())
+        return 0
+
+    lax.fori_loop(0, H, end_q, 0)
 
     def end(u, _):
         give(u, lambda c: c.wait_send())
@@ -272,11 +305,10 @@
         scratch_shapes=[
             pltpu.VMEM((H, R2, WIDE), bf),
             pltpu.VMEM((H, R, WIDE), bf),
-            pltpu.VMEM((max(G - 1, 1), hg, R2, WIDE), bf),
             pltpu.VMEM((max(G - 1, 1), hg, R, WIDE), bf),
             pltpu.VMEM((H, R2, WIDE), bf),
             pltpu.VMEM((NS, B, R, WIDE), bf),
-            pltpu.VMEM((NS, B // G, R, WIDE), bf),
+            pltpu.VMEM((NS, B, R, WIDE), bf),
             pltpu.VMEM((H, R, WIDE), bf),
             pltpu.VMEM((H, R, WIDE), f32),
             pltpu.VMEM((H, R, WIDE), f32),
@@ -284,9 +316,9 @@
             pltpu.VMEM((H, R2, WIDE), bf),
             pltpu.VMEM((R, features), bf),
             pltpu.VMEM(out_weight.shape, bf),
-            dma((max(G - 1, 1), 2)),
-            dma((max(G - 1, 1), 2)),
-            dma((G, hg)),
+            dma((max(G - 1, 1),)),
+            dma((max(G - 1, 1),)),
+            dma((H,)),
             dma((H,)),
             dma((G, B // G, NS)),
             dma((NS, B)),
@@ -295,7 +327,7 @@
             dma(()),
         ],
         compiler_params=pltpu.CompilerParams(
-            has_side_effects=True, vmem_limit_bytes=60 * 1024 * 1024
+            collective_id=0, has_side_effects=True, vmem_limit_bytes=60 * 1024 * 1024
         ),
         name="attention",
     )(query, key, value, out_weight)

time: 79.6 us -> 69.4 us (0.87)
  Pallas kernels: 77.3 us -> 66.7 us
    pallas_call x1, Pallas kernels: 77.3 us -> 66.7 us  [per_device(): pl.pallas_call(functools.partial(kernel, G, B, N), out_shape=jax.ShapeDty...]
where the time goes in v3:
time: 69.4 us; the launch traced here: 68.4 us
  Pallas kernels  66.7 us (96%)
  local copies, waits for them, and re-layouts  1.75 us (3%)
    pallas_call x1, Pallas kernels, per_device(): pl.pallas_call(functools.partial(kernel, G, B, N), out_shape=jax.ShapeDty...  66.7 us
    unnamed x1, local copies, waits for them, and re-layouts  1.75 us

profile of v3, /device:TPU:3, one launch (start us, length us, event | category | flops | bytes accessed | tf_op | source)
XLA Modules:
  0.0 68.4 jit_solution(14208158169416235444)
XLA Ops:
  0.0 66.7 %attention.1 = bf16[144,1280]{1,0:T(8,128)(2,1)} custom-call(bf16[144,1280]{1,0:T(8,128)(2,1)} %query_ref.1, bf16[144,1280]{1,0:T(8,128)(2,1)} %key_ref.1, bf16[144,1280]{1,0:T(8,128)(2,1)} %value_ref.1, bf16[1280,1280]{1,0:T(8,128)(2,1)} %weight_ref.1), custom_call_target="tpu_custom_call" | custom-call | tf_op jit(solution)/shard_map/attention/pallas_call | solution.py:300
  66.7 1.7 %copy.6 = bf16[144,1280]{1,0:T(8,128)(2,1)} copy(bf16[144,1280]{1,0:T(8,128)(2,1)} %attention.1) | data formatting | bytes 737280

commit v4 on v3

--- a/solution.py
+++ b/solution.py
@@ -231,29 +231,28 @@
             share_kv(s, start)
             own_kv(s)
 
-    stages = [(s, s + 1) for s in range(min(G, 2))]
-    stages += [(s, min(s + 2, G)) for s in range(2, G, 2)]
+    stages = [(0, 1)] + [(s, min(s + 2, G)) for s in range(1, G, 2)]
     turns = H // C
     relay(1)
+    relayed = 2
     lax.fori_loop(0, H, take_q, 0)
     for low, high in stages:
+        while relayed < high:
+            relay(relayed)
+            relayed += 1
         take_kv(low, high)
 
         def turn(t, _):
             attend(low, high, t)
             return 0
 
-        if high == 2 and low == 1 and G > 3:
+        if low > 0 and high < G:
             lax.fori_loop(0, turns // 2, turn, 0)
-            relay(3)
+            relay(relayed)
+            relayed += 1
             lax.fori_loop(turns // 2, turns, turn, 0)
         else:
             lax.fori_loop(0, turns, turn, 0)
-        if high == 1:
-            relay(2)
-        if high >= 2:
-            for s in range(high + 2, min(high + 4, G)):
-                relay(s)
 
     for dz in range(1, G):
         phase1(dz).wait_send()

time: 69.4 us -> 72.4 us (1.043)
  Pallas kernels: 66.7 us -> 69.7 us
    pallas_call x1, Pallas kernels: 66.7 us -> 69.7 us  [per_device(): pl.pallas_call(functools.partial(kernel, G, B, N), out_shape=jax.ShapeDty...]
where the time goes in v4:
time: 72.4 us; the launch traced here: 71.4 us
  Pallas kernels  69.7 us (96%)
  local copies, waits for them, and re-layouts  1.75 us (2%)
    pallas_call x1, Pallas kernels, per_device(): pl.pallas_call(functools.partial(kernel, G, B, N), out_shape=jax.ShapeDty...  69.7 us
    unnamed x1, local copies, waits for them, and re-layouts  1.75 us

profile of v4, /device:TPU:3, one launch (start us, length us, event | category | flops | bytes accessed | tf_op | source)
XLA Modules:
  0.0 71.4 jit_solution(16746674730070758310)
XLA Ops:
  0.0 69.7 %attention.1 = bf16[144,1280]{1,0:T(8,128)(2,1)} custom-call(bf16[144,1280]{1,0:T(8,128)(2,1)} %query_ref.1, bf16[144,1280]{1,0:T(8,128)(2,1)} %key_ref.1, bf16[144,1280]{1,0:T(8,128)(2,1)} %value_ref.1, bf16[1280,1280]{1,0:T(8,128)(2,1)} %weight_ref.1), custom_call_target="tpu_custom_call" | custom-call | tf_op jit(solution)/shard_map/attention/pallas_call | solution.py:299
  69.7 1.7 %copy.6 = bf16[144,1280]{1,0:T(8,128)(2,1)} copy(bf16[144,1280]{1,0:T(8,128)(2,1)} %attention.1) | data formatting | bytes 737280
